TPU v7x, 32 devices: a whole 2x2x4 slice. The times are simulated.
32 devices in a mesh: row: 4 (over y, core), col: 8 (over z, x).
Axes of the slice: x: 2, y: 2, z: 4, core: 2. Of those that a mesh axis runs over, the one named last changes fastest.
Arguments:
- hidden_acts: bfloat16 [256, 29568], P('row', 'col'), may hold values from -6 to 6
- output_errors: bfloat16 [256, 4096], P('col', 'row'), may hold values from -6 to 6
- col_points: int32 [8], replicated, may hold values from 0 to 16, as said below
- row_points: int32 [4], replicated, may hold values from 0 to 8, as said below
- worker_mask: int32 [4, 8], replicated, may hold values from 0 to 1, as said below
Outputs:
- clipped_grad: float32 [2, 2048, 29568], P(None, 'col', 'row')
Inputs may be any that keep to these rules, and one draw needn't show every extreme that they name: `col_points`: distinct node indices. `row_points`: distinct node indices. `worker_mask`: each row of the grid has between 1 and 2 erased workers.
All inputs are finite; a program needn't handle non-finite values.
Results may differ from a plain program's by a relative error of at most 0.02.
Values may be sent and summed in bfloat16 or wider, within the bound.
A program may use at most 192 MiB of HBM per device.

v0:
```python
import jax
import jax.numpy as jnp
from jax import lax
from jax.sharding import PartitionSpec as P

D = 4096
FF = 29568


def node_value(index, count):
    return jnp.cos(jnp.pi * (2.0 * index.astype(jnp.float32) + 1.0) / (2.0 * count))


def berrut(nodes, signs, live, targets):
    terms = (live * signs)[:, None] / (targets[None, :] - nodes[:, None])
    return terms / jnp.sum(terms, axis=0, keepdims=True)


def rank_signs(points, live):
    lower = (points[None, :] < points[:, None]).astype(jnp.int32)
    ranks = jnp.sum(lower * live[None, :], axis=1)
    return (1 - 2 * (ranks % 2)).astype(jnp.float32)


def encode_blocks(source, weights, block_count, block_width):

    def add_block(index, total):
        piece = lax.dynamic_slice_in_dim(source, index * block_width, block_width, 1).astype(
            jnp.float32
        )
        factor = lax.dynamic_slice_in_dim(weights, index, 1, 0)
        return total + factor * piece

    start = jnp.zeros((source.shape[0], block_width), jnp.float32)
    return lax.fori_loop(0, block_count, add_block, start).astype(jnp.bfloat16)


def shards(hidden_acts, output_errors, col_points, row_points, worker_mask):
    col_count = lax.axis_size("col")
    row_count = lax.axis_size("row")
    col_place = lax.axis_index("col")
    row_place = lax.axis_index("row")
    act_blocks = col_count // 2
    err_blocks = row_count // 2
    act_width = FF // act_blocks
    err_width = D // err_blocks
    data_acts = node_value(jnp.arange(act_blocks), act_blocks)
    data_errs = node_value(jnp.arange(err_blocks), err_blocks)
    work_acts = node_value(col_points, 2 * col_count + 1)
    work_errs = node_value(row_points, 2 * row_count + 1)
    alt_acts = (1 - 2 * (jnp.arange(act_blocks) % 2)).astype(jnp.float32)
    alt_errs = (1 - 2 * (jnp.arange(err_blocks) % 2)).astype(jnp.float32)
    full_acts = lax.all_gather(hidden_acts, "col", axis=1, tiled=True)
    own_node = lax.dynamic_slice_in_dim(work_acts, col_place, 1, 0)
    encode_own = berrut(data_acts, alt_acts, jnp.ones((act_blocks,), jnp.float32), own_node)[:, 0]
    coded_acts = encode_blocks(full_acts, encode_own, act_blocks, act_width)
    full_errs = lax.all_gather(output_errors, "row", axis=1, tiled=True)
    own_err = lax.dynamic_slice_in_dim(work_errs, row_place, 1, 0)
    encode_err = berrut(data_errs, alt_errs, jnp.ones((err_blocks,), jnp.float32), own_err)[:, 0]
    coded_errs = encode_blocks(full_errs, encode_err, err_blocks, err_width)
    all_errs = lax.all_gather(coded_errs, "col", axis=0, tiled=True)
    product = lax.dot_general(
        all_errs,
        lax.all_gather(coded_acts, "row", axis=0, tiled=True),
        (((0,), (0,)), ((), ())),
        preferred_element_type=jnp.float32,
    ).astype(jnp.bfloat16)
    live = lax.dynamic_slice_in_dim(worker_mask, row_place, 1, 0)[0]
    decode_acts = berrut(
        work_acts, rank_signs(col_points, live), live.astype(jnp.float32), data_acts
    )
    decoded = jnp.einsum(
        "jk,jrf->rkf",
        decode_acts,
        lax.all_to_all(product[None], "col", split_axis=1, concat_axis=0, tiled=True).astype(
            jnp.float32
        ),
    ).astype(jnp.bfloat16)
    decoded = decoded.reshape(decoded.shape[0], FF)
    all_rows = jnp.ones((row_count,), jnp.int32)
    decode_errs = berrut(
        work_errs, rank_signs(row_points, all_rows), jnp.ones((row_count,), jnp.float32), data_errs
    )
    grad = jnp.einsum(
        "il,irf->lrf",
        decode_errs,
        lax.all_to_all(decoded[None], "row", split_axis=2, concat_axis=0, tiled=True).astype(
            jnp.float32
        ),
    )
    squares = lax.psum(jnp.sum(grad * grad), ("row", "col"))
    factor = jnp.minimum(1.0, jnp.sqrt(jnp.float32(FF * D)) / jnp.sqrt(squares + 1e-06))
    return grad * factor


def solution(mesh):
    return jax.shard_map(
        shards,
        mesh=mesh,
        in_specs=(P("row", "col"), P("col", "row"), P(), P(), P()),
        out_specs=P(None, "col", "row"),
        check_vma=False,
    )
```

profile of v0, /device:TPU:12, one launch (start us, length us, event | category | flops | bytes accessed | tf_op | source)
XLA Modules:
  0.0 2220.5 jit_solution(384368010853941417)
XLA Ops:
  10.0 6.0 all_gather.12
  17.2 2.7 while.28
  26.3 52.1 %all-gather.9.cloned.1.call-done = bf16[8,3696,64]{1,2,0:T(8,128)(2,1)} async-done(((bf16[1,3696,64]{1,2,0:T(8,128)(2,1)}), bf16[8,3696,64]{1,2,0:T(8,128)(2,1)}) %all-gather.9.cloned.1.call-update) | async-done | bytes 3784720 | tf_op jit(solution)/shard_map/all_gather | solution.py:53
  78.4 6.1 copy.25
  84.5 6.8 reshape.100
  91.2 12.4 while.29
  91.8 2.5 select_add_fusion.5
  94.9 2.5 select_add_fusion.5
  104.7 13.8 all-gather.5.cloned.1.call-done
  118.5 32.8 %all-gather.7.cloned.1.call-done = bf16[256,7392]{1,0:T(8,128)(2,1)} async-done(((bf16[64,7392]{1,0:T(8,128)(2,1)}), bf16[256,7392]{1,0:T(8,128)(2,1)}) %all-gather.7.cloned.1.call-update) | async-done | bytes 3784720 | tf_op jit(solution)/shard_map/all_gather | solution.py:64
  151.2 15.0 convert_bitcast_fusion
  166.2 123.4 %copy.26 = bf16[1,2048,7392]{2,0,1:T(2,128)(2,1)} copy(bf16[1,2048,7392]{1,2,0:T(8,128)(2,1)} %convert_bitcast_fusion) | data formatting | bytes 60555264 | tf_op jit(solution)/shard_map/broadcast_in_dim | solution.py:75
  290.1 188.5 %reduce.2 = bf16[2048,7392]{1,0:T(8,128)(2,1)} reduce(bf16[2048,1,7392]{2,1,0:T(2,128)(2,1)} %bitcast.51, bf16[]{:T(256)} %broadcast.331), dimensions={1}, to_apply=%bitcast.30.reduce_sub_computation | reduce | bytes 60555264
  478.6 48.8 %reshape.104 = bf16[8,2,946176]{2,1,0:T(2,128)(2,1)} reshape(bf16[2048,7392]{1,0:T(8,128)(2,1)} %reduce.2) | data formatting | bytes 60555264
  527.4 7.2 all-to-all-start
  534.8 650.2 %all-to-all-done = bf16[8,2,946176]{2,1,0:T(2,128)(2,1)} async-done(((bf16[8,2,946176]{2,1,0:T(2,128)(2,1)}), bf16[8,2,946176]{2,1,0:T(2,128)(2,1)}, u32[]{:S(2)}, u32[]{:S(2)}) %all-to-all-start) | async-done | bytes 30277664 | tf_op jit(solution)/shard_map/all_to_all | solution.py:75
  1185.0 86.2 %reshape.105 = bf16[2048,1,7392]{2,1,0:T(2,128)(2,1)} reshape(bf16[8,2,946176]{2,1,0:T(2,128)(2,1)} %all-to-all-done) | data formatting | bytes 60555264
  1271.2 30.4 %copy.33 = bf16[1,2048,7392]{2,1,0:T(8,128)(2,1)} copy(bf16[1,2048,7392]{2,0,1:T(2,128)(2,1)} %bitcast.52) | data formatting | bytes 60555264
  1301.6 39.8 %copy.32 = bf16[8,256,7392]{1,0,2:T(8,128)(2,1)} copy(bf16[8,256,7392]{2,1,0:T(8,128)(2,1)} %bitcast.53) | data formatting | bytes 60555264 | tf_op jit(solution)/shard_map/all_to_all | solution.py:75
  1341.4 17.5 convert_bitcast_fusion.1
  1358.9 9.0 copy.28
  1367.8 176.9 %copy.42 = bf16[1,256,29568]{1,0,2:T(2,128)(2,1)} copy(bf16[1,256,29568]{1,2,0:T(8,128)(2,1)S(1)} %bitcast.56) | data formatting | bytes 30277632 | tf_op jit(solution)/shard_map/broadcast_in_dim;reshape | solution.py:87
  1544.7 322.2 %reduce.3 = bf16[29568,256]{1,0:T(8,128)(2,1)} reduce(bf16[29568,1,256]{2,1,0:T(2,128)(2,1)} %bitcast.54, bf16[]{:T(256)} %broadcast.331), dimensions={1}, to_apply=%bitcast.44.reduce_sub_computation | reduce | bytes 30277634
  1866.9 12.2 reshape.106
  1879.1 8.4 all-to-all-start.1
  1888.0 163.4 %all-to-all-done.1 = bf16[4,2,946176]{2,1,0:T(2,128)(2,1)} async-done(((bf16[4,2,946176]{2,1,0:T(2,128)(2,1)}), bf16[4,2,946176]{2,1,0:T(2,128)(2,1)}, u32[]{:S(2)}, u32[]{:S(2)}) %all-to-all-start.1) | async-done | bytes 15138848 | tf_op jit(solution)/shard_map/all_to_all | solution.py:87
  2051.5 33.1 %reshape.107 = bf16[29568,1,256]{2,1,0:T(2,128)(2,1)} reshape(bf16[4,2,946176]{2,1,0:T(2,128)(2,1)} %all-to-all-done.1) | data formatting | bytes 30277632
  2084.6 18.8 copy.34
  2103.4 44.4 %multiply_reduce_fusion = (f32[]{:T(128)}, f32[2,256,7392]{1,0,2:T(2,128)}) fusion(bf16[1,256,4,7392]{1,3,2,0:T(8,128)(2,1)} %bitcast.59, f32[2]{0:T(128)S(1)} %fusion.7, f32[4]{0:T(128)S(1)} %copy-done.1, f32[4]{0:T(128)S(1)} %fusion.17, f32[2]{0:T(128)S(1)} %multiply_cosine_fusion.3), kind=kOutput, calls=%fused_computation.6 | convolution fusion | flops 37847064 | bytes 30277684 | tf_op jit(solution)/shard_map/il,irf->lrf/dot_general | solution.py:84
  2147.7 42.6 %psum.7 = f32[]{:T(128)} all-reduce(f32[]{:T(128)} %get-tuple-element.211), channel_id=1, replica_groups=mesh['row'=4,'col'=8] {'row','col'}, use_global_device_ids=true, to_apply=%region_11.12 | all-reduce | flops 1 | bytes 8 | tf_op jit(solution)/shard_map/psum | solution.py:91
  2191.0 10.6 broadcast_multiply_fusion
  2201.6 12.1 copy.31
  (43 shorter events, 23.2 us)
Async XLA Ops:
  6.5 71.9 %all-gather.9.cloned.1.call-start = ((), (), s32[]{:S(2)}) async-start(), calls=%async_computation.4 | async-start | bytes 4276224 | tf_op jit(solution)/shard_map/all_gather | solution.py:53
  7.3 111.2 %all-gather.5.cloned.1.call-start = ((), (), s32[]{:S(2)}) async-start(), calls=%async_computation.2 | async-start | bytes 1179648 | tf_op jit(solution)/shard_map/all_gather | solution.py:61
  8.0 0.7 copy-start
  20.6 130.6 %all-gather.7.cloned.1.call-start = ((), (), s32[]{:S(2)}) async-start(), calls=%async_computation.3 | async-start | bytes 4751360 | tf_op jit(solution)/shard_map/all_gather | solution.py:64
  527.4 657.6 %all-to-all-start = ((bf16[8,2,946176]{2,1,0:T(2,128)(2,1)}), bf16[8,2,946176]{2,1,0:T(2,128)(2,1)}, u32[]{:S(2)}, u32[]{:S(2)}) async-start(bf16[8,2,946176]{2,1,0:T(2,128)(2,1)} %reshape.104), calls=%async_computation | async-start | bytes 60555264 | tf_op jit(solution)/shard_map/all_to_all | solution.py:75
  1879.1 8.5 copy-start.2
  1879.1 8.7 copy-start.1
  1879.1 172.3 %all-to-all-start.1 = ((bf16[4,2,946176]{2,1,0:T(2,128)(2,1)}), bf16[4,2,946176]{2,1,0:T(2,128)(2,1)}, u32[]{:S(2)}, u32[]{:S(2)}) async-start(bf16[4,2,946176]{2,1,0:T(2,128)(2,1)} %reshape.106), calls=%async_computation.1 | async-start | bytes 30277632 | tf_op jit(solution)/shard_map/all_to_all | solution.py:87
Sparse Core Ops, SparseCore 0:
  9.5 68.8 all-gather.8
  80.5 37.8 all-gather.4
  120.0 31.1 all-gather.6
where the time goes:
time: 2230 us; the launch traced here: 2220 us
  waiting for transfers between devices  913 us (41%)
  local copies, waits for them, and re-layouts  610 us (27%)
  other arithmetic  543 us (24%)
  matrix products  76.8 us (3%)
  blocking collectives  48.6 us (2%)
    all_to_all x1, waiting for transfers between devices, shards(): lax.all_to_all(product[None], 'col', split_axis=1, concat_axis=0, tiled=T...  650 us
    unnamed x4, other arithmetic  511 us
    unnamed x14, local copies, waits for them, and re-layouts  237 us
    another operation x1, local copies, waits for them, and re-layouts, shards(): decoded[None]  177 us
    all_to_all x1, waiting for transfers between devices, shards(): lax.all_to_all(decoded[None], 'row', split_axis=2, concat_axis=0, tiled=T...  163 us
    broadcast_in_dim x1, local copies, waits for them, and re-layouts, shards(): product[None]  123 us
    all_gather x1, waiting for transfers between devices, shards(): full_acts = lax.all_gather(hidden_acts, 'col', axis=1, tiled=True)  52.1 us
  transfers between devices with their start and end apart: 5, of which 5 were waited for; matrix products, arithmetic and copies ran while one was open for 2% of the time, Pallas kernels for 0%

commit v1 on v0

v1 whole, which is shorter than its diff:
```python
import functools

import jax
import jax.numpy as jnp
from jax import lax
from jax.experimental import pallas as pl
from jax.experimental.pallas import tpu as pltpu
from jax.sharding import PartitionSpec as P

LANES = 128


def node_value(index, count):
    return jnp.cos(jnp.pi * (2.0 * index.astype(jnp.float32) + 1.0) / (2.0 * count))


def berrut(nodes, signs, live, targets):
    terms = (live * signs)[..., :, None] / (targets[None, :] - nodes[:, None])
    return terms / jnp.sum(terms, axis=-2, keepdims=True)


def rank_signs(points, live):
    lower = (points[None, :] < points[:, None]).astype(jnp.int32)
    ranks = jnp.sum(lower * live[..., None, :], axis=-1)
    return (1 - 2 * (ranks % 2)).astype(jnp.float32)


def mixing(col_points, row_points, worker_mask, act_blocks, err_blocks, block):
    row_count, col_count = worker_mask.shape
    data_acts = node_value(jnp.arange(act_blocks), act_blocks)
    data_errs = node_value(jnp.arange(err_blocks), err_blocks)
    work_acts = node_value(col_points, 2 * col_count + 1)
    work_errs = node_value(row_points, 2 * row_count + 1)
    alt_acts = (1 - 2 * (jnp.arange(act_blocks) % 2)).astype(jnp.float32)
    alt_errs = (1 - 2 * (jnp.arange(err_blocks) % 2)).astype(jnp.float32)
    encode_acts = berrut(data_acts, alt_acts, jnp.ones((act_blocks,), jnp.float32), work_acts)
    encode_errs = berrut(data_errs, alt_errs, jnp.ones((err_blocks,), jnp.float32), work_errs)
    all_rows = jnp.ones((row_count,), jnp.int32)
    decode_errs = berrut(
        work_errs, rank_signs(row_points, all_rows), all_rows.astype(jnp.float32), data_errs
    )
    target = lax.dynamic_slice_in_dim(data_acts, block, 1, 0)
    decode_acts = berrut(
        work_acts, rank_signs(col_points, worker_mask), worker_mask.astype(jnp.float32), target
    )[..., 0]
    through = jnp.sum(decode_acts[:, None, :] * encode_acts[None], axis=-1)
    return jnp.sum(
        decode_errs.T[:, None, None, :] * encode_errs[None, :, None, :] * through.T[None, None],
        axis=-1,
    )


def place_in_tiles(piece, part, parts, chunk):
    width = piece.shape[1]
    placed = None
    for index in range(parts):
        shift = index * width % LANES
        here = jnp.pad(piece, ((0, 0), (shift, chunk - shift - width)))
        placed = here if placed is None else jnp.where(part == index, here, placed)
    return placed


def product_kernel(bases, step, mix_ref, acts_ref, grad_ref, square_ref):
    part, tile = pl.program_id(0), pl.program_id(1)
    lead, groups, width = grad_ref.shape
    rows = lead * groups
    depth = acts_ref.shape[0] * acts_ref.shape[1]
    result = jnp.dot(
        mix_ref[...], acts_ref[...].reshape(depth, step), preferred_element_type=jnp.float32
    )
    for index, base in enumerate(bases):
        for turn in range(pl.num_programs(1)):
            start = base + turn * step

            @pl.when((part == index) & (tile == turn))
            def _():
                size = min(step, width - start)
                shared = LANES if index > 0 and turn == 0 else 0
                for block in range(lead):
                    here = result[block * groups : (block + 1) * groups]
                    if shared:
                        grad_ref[block, :, start : start + shared] += here[:, :shared]
                    grad_ref[block, :, start + shared : start + size] = here[:, shared:size]

    @pl.when((part == len(bases) - 1) & (tile == pl.num_programs(1) - 1))
    def _():
        strip = 8

        def add(index, total):
            for block in range(lead):
                piece = grad_ref[block, pl.ds(pl.multiple_of(index * strip, strip), strip), :]
                total = total + piece * piece
            return total

        total = lax.fori_loop(0, groups // strip, add, jnp.zeros((strip, width), jnp.float32))
        square_ref[0, 0] = jnp.sum(total)


def scale_kernel(factor_ref, grad_ref, out_ref, stage, sem):
    lead, groups, width = grad_ref.shape
    strip = stage.shape[1]
    count = lead * groups // strip
    per = groups // strip

    def copy(index, slot):
        return pltpu.make_async_copy(
            stage.at[slot],
            out_ref.at[index // per, pl.ds(pl.multiple_of(index % per * strip, strip), strip), :],
            sem.at[slot],
        )

    @pl.loop(0, count)
    def _(index):
        slot = index % 4

        @pl.when(index >= 4)
        def _():
            copy(index - 4, slot).wait()

        stage[slot] = (
            grad_ref[index // per, pl.ds(pl.multiple_of(index % per * strip, strip), strip), :]
            * factor_ref[0]
        )
        copy(index, slot).start()

    for index in range(count - 4, count):
        copy(index, index % 4).wait()


def solution(mesh):
    row_count, col_count = mesh.shape["row"], mesh.shape["col"]
    act_blocks, err_blocks = col_count // 2, row_count // 2
    parts = col_count // act_blocks
    assert act_blocks == row_count

    def shards(hidden_acts, output_errors, col_points, row_points, worker_mask):
        row_place, col_place = lax.axis_index("row"), lax.axis_index("col")
        width = hidden_acts.shape[1]
        tokens = hidden_acts.shape[0] * row_count
        act_width = width * parts
        bases = [part * width // LANES * LANES for part in range(parts)]
        chunk = max(
            -(-((part + 1) * width - base) // LANES) * LANES for part, base in enumerate(bases)
        )
        groups = output_errors.shape[1] * row_count // err_blocks // col_count
        acts = lax.all_gather(
            place_in_tiles(hidden_acts, col_place % parts, parts, chunk),
            ("col", "row"),
            axis=0,
            tiled=True,
        ).reshape(act_blocks, parts, tokens, chunk)

        errs = lax.all_gather(output_errors, "row", axis=1, tiled=True)
        errs = errs.reshape(errs.shape[0], err_blocks, col_count, groups)
        errs = lax.all_to_all(errs, "col", split_axis=2, concat_axis=0, tiled=True)[:, :, 0]
        mix = mixing(col_points, row_points, worker_mask, act_blocks, err_blocks, row_place)
        source = errs.astype(jnp.float32)
        left = sum(
            mix[:, m, :, None, None] * source[:, m].T[None, None] for m in range(err_blocks)
        )
        left = left.astype(jnp.bfloat16)
        left = left.transpose(0, 2, 1, 3).reshape(err_blocks * groups, act_blocks * tokens)

        tiles = chunk // LANES
        step = LANES * max(n for n in range(1, 7) if tiles % n == 0)
        shape = (err_blocks, groups, act_width)
        grad, squares = pl.pallas_call(
            functools.partial(product_kernel, bases, step),
            grid=(parts, chunk // step),
            in_specs=[
                pl.BlockSpec(left.shape, lambda part, tile: (0, 0)),
                pl.BlockSpec(
                    (act_blocks, None, tokens, step), lambda part, tile: (0, part, 0, tile)
                ),
            ],
            out_specs=[
                pl.BlockSpec(memory_space=pltpu.VMEM),
                pl.BlockSpec(memory_space=pltpu.SMEM),
            ],
            out_shape=[
                pltpu.VMEM(shape, jnp.float32),
                jax.ShapeDtypeStruct((1, 1), jnp.float32),
            ],
            compiler_params=pltpu.CompilerParams(vmem_limit_bytes=40 * 2**20),
            cost_estimate=pl.CostEstimate(
                flops=4 * left.size * act_width,
                bytes_accessed=acts.size * 2,
                transcendentals=0,
            ),
            name="product",
        )(left, acts)
        squares = lax.psum(squares[0, 0], ("row", "col"))
        size = shape[0] * shape[1] * shape[2] * row_count * col_count
        factor = jnp.minimum(1.0, jnp.sqrt(jnp.float32(size)) / jnp.sqrt(squares + 1e-06))
        strip = min(32, groups)
        return pl.pallas_call(
            scale_kernel,
            in_specs=[
                pl.BlockSpec(memory_space=pltpu.SMEM),
                pl.BlockSpec(memory_space=pltpu.VMEM),
            ],
            out_specs=pl.BlockSpec(memory_space=pl.ANY),
            out_shape=jax.ShapeDtypeStruct(shape, jnp.float32),
            scratch_shapes=[
                pltpu.VMEM((4, strip, act_width), jnp.float32),
                pltpu.SemaphoreType.DMA((4,)),
            ],
            compiler_params=pltpu.CompilerParams(vmem_limit_bytes=40 * 2**20),
            name="scale",
        )(factor[None], grad)

    return jax.shard_map(
        shards,
        mesh=mesh,
        in_specs=(P("row", "col"), P("col", "row"), P(), P(), P()),
        out_specs=P(None, "col", "row"),
        check_vma=False,
    )
```

time: 2230 us -> 224 us (0.10)
  waiting for transfers between devices: 913 us -> 98.5 us
  local copies, waits for them, and re-layouts: 610 us -> 23.7 us
  other arithmetic: 543 us -> 4.94 us
  matrix products: 76.8 us -> 0 us
  Pallas kernels: 0 us -> 28.3 us
    all_to_all x2 -> x1, waiting for transfers between devices: 814 us -> 11.4 us  [shards(): lax.all_to_all(errs, 'col', split_axis=2, concat_axis=0, tiled=True)]
    unnamed x4 -> x0, other arithmetic: 511 us -> none
    unnamed x14 -> x10, local copies, waits for them, and re-layouts: 237 us -> 6.59 us
    another operation x1 -> x0, local copies, waits for them, and re-layouts: 177 us -> none  [shards(): decoded[None]]
    broadcast_in_dim x1 -> x0, local copies, waits for them, and re-layouts: 123 us -> none  [shards(): product[None]]
    dot_general x3 -> x0, matrix products: 76.8 us -> none  [the longest x1 44.4 us: shards(): jnp.einsum('il,irf->lrf', decode_errs, lax.all_to_all(decoded[None], 'row...]
    all_to_all x1 -> x0, local copies, waits for them, and re-layouts: 39.8 us -> none  [shards(): lax.all_to_all(product[None], 'col', split_axis=1, concat_axis=0, tiled=T...]
    pallas_call x0 -> x2, Pallas kernels: none -> 28.3 us  [the longest x1 17.5 us: shards(): pl.pallas_call(functools.partial(product_kernel, bases, step), grid=(part...]
  transfers between devices with their start and end apart: 5 -> 2, of which waited for: 5 -> 2; matrix products, arithmetic and copies ran while one was open for 2% -> 3% of each run, Pallas kernels for 0% -> 0%
where the time goes in v1:
time: 224 us; the launch traced here: 222 us
  waiting for transfers between devices  98.5 us (44%)
  blocking collectives  46.1 us (21%)
  Pallas kernels  28.3 us (13%)
  local copies, waits for them, and re-layouts  23.7 us (11%)
  between operations  14.2 us (6%)
  starting transfers between devices  6.25 us (3%)
  other arithmetic  4.94 us (2%)
    all_gather x1, waiting for transfers between devices, shards(): lax.all_gather(place_in_tiles(hidden_acts, col_place % parts, parts, chun...  87.2 us
    psum x1, blocking collectives, shards(): squares = lax.psum(squares[0, 0], ('row', 'col'))  40.1 us
    pallas_call x1, Pallas kernels, shards(): pl.pallas_call(functools.partial(product_kernel, bases, step), grid=(part...  17.5 us
    pallas_call x1, local copies, waits for them, and re-layouts, shards(): pl.pallas_call(scale_kernel, in_specs=[pl.BlockSpec(memory_space=pltpu.SM...  15.3 us
    all_to_all x1, waiting for transfers between devices, shards(): lax.all_to_all(errs, 'col', split_axis=2, concat_axis=0, tiled=True)  11.4 us
    pallas_call x1, Pallas kernels, shards(): pl.pallas_call(scale_kernel, in_specs=[pl.BlockSpec(memory_space=pltpu.SM...  10.8 us
    unnamed x10, local copies, waits for them, and re-layouts  6.59 us
    all_to_all x1, starting transfers between devices, shards(): lax.all_to_all(errs, 'col', split_axis=2, concat_axis=0, tiled=True)  6.25 us
  transfers between devices with their start and end apart: 2, of which 2 were waited for; matrix products, arithmetic and copies ran while one was open for 3% of the time, Pallas kernels for 0%

profile of v1, /device:TPU:12, one launch (start us, length us, event | category | flops | bytes accessed | tf_op | source)
XLA Modules:
  0.0 222.0 jit_solution(3942180306713780426)
XLA Ops:
  6.5 2.2 pad_select_fusion
  8.8 0.0 all-gather.2.cloned.1.call-update
  8.8 6.0 %all_gather.6 = bf16[32,4096]{1,0:T(8,128)(2,1)S(1)} all-gather(bf16[32,1024]{1,0:T(8,128)(2,1)} %param.6), channel_id=1, replica_groups=mesh['row'=4,'col'=8] {'row'}, dimensions={1}, use_global_device_ids=true | all-gather | bytes 327680 | tf_op jit(solution)/shard_map/all_gather | solution.py:153
  14.8 0.9 copy.20
  15.7 6.3 %all-to-all-start = ((bf16[32,2,8,256]{3,1,0,2:T(2,128)(2,1)}), bf16[32,2,8,256]{3,1,0,2:T(2,128)(2,1)S(1)}, u32[]{:S(2)}, u32[]{:S(2)}) async-start(bf16[32,2,8,256]{3,1,0,2:T(2,128)(2,1)} %copy.20), calls=%async_computation | async-start | bytes 524288 | tf_op jit(solution)/shard_map/all_to_all | solution.py:155
  22.0 0.6 dynamic_slice.3
  22.6 0.1 compare_convert_fusion
  22.7 0.1 multiply_reduce_fusion
  22.8 0.7 broadcast_subtract_fusion
  23.5 0.1 divide_reduce_fusion
  23.6 0.1 fusion
  23.7 0.1 fusion.1
  23.8 0.1 multiply_reduce_fusion.2
  23.9 0.1 copy.19
  24.0 0.1 multiply_cosine_fusion.3
  24.1 0.2 convert_reduce_fusion
  24.3 0.2 fusion.9
  24.5 0.1 multiply_divide_fusion.1
  24.6 0.1 fusion.8
  24.7 0.1 multiply_reduce_fusion.1
  24.8 11.4 %all-to-all-done = bf16[32,2,8,256]{3,1,0,2:T(2,128)(2,1)S(1)} async-done(((bf16[32,2,8,256]{3,1,0,2:T(2,128)(2,1)}), bf16[32,2,8,256]{3,1,0,2:T(2,128)(2,1)S(1)}, u32[]{:S(2)}, u32[]{:S(2)}) %all-to-all-start) | async-done | bytes 262176 | tf_op jit(solution)/shard_map/all_to_all | solution.py:155
  36.1 0.1 bitcast_convert_fusion
  36.3 0.1 copy.22
  36.4 0.1 copy.23
  36.5 0.6 add_convert_fusion
  37.1 1.2 copy.26
  38.3 87.2 %all-gather.2.cloned.1.call-done = bf16[2048,3840]{1,0:T(8,128)(2,1)} async-done(((bf16[64,3840]{1,0:T(8,128)(2,1)}), bf16[2048,3840]{1,0:T(8,128)(2,1)}) %all-gather.2.cloned.1.call-update) | async-done | bytes 15728656 | tf_op jit(solution)/shard_map/all_gather | solution.py:146
  125.5 17.5 %product.1 = (f32[2,256,7392]{2,1,0:T(8,128)S(1)}, f32[1,1]{1,0:T(1,128)}) custom-call(bf16[512,1024]{1,0:T(8,128)(2,1)} %bitcast.30, bf16[4,2,256,3840]{3,2,1,0:T(8,128)(2,1)} %bitcast.35), custom_call_target="tpu_custom_call" | custom-call | flops 15502147584 | bytes 15728640 | tf_op jit(solution)/shard_map/product/pallas_call | solution.py:167
  143.0 5.3 %copy-done = f32[2,256,7392]{2,1,0:T(8,128)} copy-done((f32[2,256,7392]{2,1,0:T(8,128)}, f32[2,256,7392]{2,1,0:T(8,128)S(1)}, u32[]{:S(2)}) %copy-start) | copy-done | bytes 15138840
  148.3 40.1 %psum.7 = f32[]{:T(128)} all-reduce(f32[]{:T(128)} %bitcast.14), channel_id=1, replica_groups=mesh['row'=4,'col'=8] {'row','col'}, use_global_device_ids=true, to_apply=%region_8.9 | all-reduce | flops 1 | bytes 8 | tf_op jit(solution)/shard_map/psum | solution.py:192
  189.2 10.8 %scale.1 = f32[2,256,7392]{2,1,0:T(8,128)} custom-call(f32[1]{0:T(128)} %bitcast.15.factor_ref, f32[2,256,7392]{2,1,0:T(8,128)} %copy-done), custom_call_target="tpu_custom_call" | custom-call | tf_op jit(solution)/shard_map/scale/pallas_call | solution.py:196
  199.9 15.3 %copy.24 = f32[2,256,7392]{1,2,0:T(8,128)} copy(f32[2,256,7392]{2,1,0:T(8,128)} %scale.1) | data formatting | bytes 30277632 | tf_op jit(solution)/shard_map/scale/pallas_call | solution.py:196
  (17 shorter events, 0.2 us)
Async XLA Ops:
  6.5 16.1 %copy-start.2 = (s32[8]{0:T(128)S(1)}, s32[8]{0:T(128)}, u32[]{:S(2)}) copy-start(s32[8]{0:T(128)} %param.7) | copy-start | bytes 100
  6.5 16.2 %copy-start.1 = (s32[4,8]{1,0:T(4,128)S(1)}, s32[4,8]{1,0:T(4,128)}, u32[]{:S(2)}) copy-start(s32[4,8]{1,0:T(4,128)} %param.9) | copy-start | bytes 388
  6.5 17.5 %copy-start.3 = (s32[4]{0:T(128)S(1)}, s32[4]{0:T(128)}, u32[]{:S(2)}) copy-start(s32[4]{0:T(128)} %param.8) | copy-start | bytes 52
  6.5 118.9 %all-gather.2.cloned.1.call-start = ((), (), s32[]{:S(2)}) async-start(), calls=%async_computation.1 | async-start | bytes 16220160 | tf_op jit(solution)/shard_map/all_gather | solution.py:146
  15.7 20.4 %all-to-all-start = ((bf16[32,2,8,256]{3,1,0,2:T(2,128)(2,1)}), bf16[32,2,8,256]{3,1,0,2:T(2,128)(2,1)S(1)}, u32[]{:S(2)}, u32[]{:S(2)}) async-start(bf16[32,2,8,256]{3,1,0,2:T(2,128)(2,1)} %copy.20), calls=%async_computation | async-start | bytes 524288 | tf_op jit(solution)/shard_map/all_to_all | solution.py:155
  143.0 5.3 %copy-start = (f32[2,256,7392]{2,1,0:T(8,128)}, f32[2,256,7392]{2,1,0:T(8,128)S(1)}, u32[]{:S(2)}) copy-start(f32[2,256,7392]{2,1,0:T(8,128)S(1)} %get-tuple-element.8.grad_ref) | copy-start | bytes 45416452
Sparse Core Ops, SparseCore 0:
  10.3 115.1 all-gather.1
